TPU v7x, 32 devices: a whole 2x2x4 slice. The times are simulated.
32 devices in a mesh: lat: 4 (over z), lon: 8 (over y, x, core).
Axes of the slice: x: 2, y: 2, z: 4, core: 2. Of those that a mesh axis runs over, the one named last changes fastest.
Arguments:
- fields: bfloat16 [3, 512, 32, 384], P(None, ('lat', 'lon')), may hold values from -6 to 6
- weights: bfloat16 [3, 1024, 8, 32, 128], P(None, ('lat', 'lon')), may hold values from -0.5 to 0.5
- pair_slots: int32 [3, 1024, 8], P(None, ('lat', 'lon')), may hold values from 0 to 15
- pair_counts: int32 [3, 1024], P(None, ('lat', 'lon')), may hold values from 1 to 8
- requests: int32 [3, 32, 16], replicated, may hold values from 0 to 511, as said below
- eofs: bfloat16 [200, 131072], P(None, ('lat', 'lon')), may hold values from -0.015625 to 0.015625
Outputs:
- pcs: float32 [200, 1152], P(None, ('lat', 'lon'))
Inputs may be any that keep to these rules, and one draw needn't show every extreme that they name: requests[g, d] lists 16 distinct source tiles for grid g and device d (d = lat index * lon devices + lon index); source tile j lies on device j // 16; all of them lie on devices with d's lat index whose lon index is d's own or one of its two cyclic neighbours, at most 8 on any one device, and exactly 8 on some device for every g and d. `pair_slots`: only entries with p < pair_counts[g, t] are used.
All inputs are finite; a program needn't handle non-finite values.
Results may differ from a plain program's by a relative error of at most 0.0029.
Values may be sent and summed in bfloat16 or wider, within the bound.
A program may use at most 128 MiB of HBM per device.

v0:
```python
import functools

import jax
import jax.numpy as jnp
from jax import lax
from jax.experimental import pallas as pl
from jax.experimental.pallas import tpu as pltpu
from jax.sharding import PartitionSpec as P

TT = 128
MONTHS = 24
LANES = 128
MESH = pl.DeviceIdType.MESH


def split_terms(value):
    high = value.astype(jnp.bfloat16)
    rest = value - high.astype(jnp.float32)
    middle = rest.astype(jnp.bfloat16)
    low = (rest - middle.astype(jnp.float32)).astype(jnp.bfloat16)
    return high, middle, low


def basis_kernel(block, tiles, slot_ref, weight_ref, eof_ref, out_ref, *totals):
    step = pl.program_id(0)
    grids, _, pairs, cells, _ = weight_ref.shape
    modes = eof_ref.shape[0]

    @pl.when(step == 0)
    def _():
        for total in totals:
            total[...] = jnp.zeros_like(total)

    for t in range(block):
        rows = weight_ref[:, t].reshape(grids * pairs * cells, TT)
        basis = eof_ref[:, t * TT:(t + 1) * TT]
        product = lax.dot_general(
            rows, basis, (((1,), (1,)), ((), ())), preferred_element_type=jnp.float32
        )
        for p in range(pairs):
            for g in range(grids):
                slot = slot_ref[(g * tiles + step * block + t) * pairs + p]
                where = pl.ds(pl.multiple_of(slot * cells, cells), cells)
                start = (g * pairs + p) * cells
                totals[g][where, :modes] += product[start:start + cells]

    @pl.when(step == pl.num_programs(0) - 1)
    def _():
        height, width = out_ref.shape[1], totals[0].shape[1]
        for g in range(grids):
            for i, term in enumerate(split_terms(totals[g][:height])):
                out_ref[g, :, i * width:(i + 1) * width] = term


def project_kernel(rel_ref, tile_ref, before_ref, own_ref, after_ref, basis_ref, out_ref, source):
    grids, _, cells, columns = own_ref.shape
    _, chips, bands, rows, _ = out_ref.shape
    wanted = rel_ref.shape[0] // grids
    width = basis_ref.shape[2] // 3
    for g in range(grids):
        for j in range(wanted):
            rel, tile = rel_ref[g * wanted + j], tile_ref[g * wanted + j]
            side = jnp.where(rel == 0, before_ref[g, tile], after_ref[g, tile])
            source[j * cells:(j + 1) * cells] = jnp.where(rel == 1, own_ref[g, tile], side)
        product = lax.dot_general(
            source[...], basis_ref[g], (((0,), (0,)), ((), ())),
            preferred_element_type=jnp.float32,
        )
        total = product[:, 2 * width:] + product[:, width:2 * width] + product[:, :width]
        months = total.reshape(columns // MONTHS, MONTHS, width)
        months = months - jnp.mean(months, axis=1, keepdims=True)
        total = months.reshape(columns, width)
        first = g * columns
        for chunk in range(chips * bands):
            low = max(chunk * rows, first)
            high = min((chunk + 1) * rows, first + columns)
            for half in range(out_ref.shape[0]):
                if low < high:
                    out_ref[
                        half, chunk % chips, chunk // chips,
                        low - chunk * rows:high - chunk * rows, :,
                    ] = total[low - first:high - first, half * LANES:(half + 1) * LANES]


def reduce_kernel(
    part_ref, out_ref, core_in, plane_sum, plane_in, band_sum, band_in, final, other,
    core_send, core_recv, plane_send, plane_recv, band_send, band_recv, last_send, last_recv,
):
    _, chips, bands, _, _ = part_ref.shape
    lat, lon = lax.axis_index("lat"), lax.axis_index("lon")
    core, chip = lax.rem(lon, 2), lon // 2
    mate = (lat, chip * 2 + 1 - core)
    plane = [(lat, lax.rem(chip + i, chips) * 2 + core) for i in range(1, chips)]
    column = [(lax.rem(lat + j, bands), lon) for j in range(1, bands)]
    barrier = pltpu.get_barrier_semaphore()
    partners = [mate] + plane + column
    for partner in partners:
        pl.semaphore_signal(barrier, inc=1, device_id=partner, device_id_type=MESH)
    pl.semaphore_wait(barrier, len(partners))

    order = list(range(1, chips)) + [0]
    band_order = list(range(1, bands)) + [0]

    def send(source, target, send_sem, recv_sem, device):
        copy = pltpu.make_async_remote_copy(
            src_ref=source, dst_ref=target, send_sem=send_sem, recv_sem=recv_sem,
            device_id=device, device_id_type=MESH,
        )
        copy.start()
        return copy

    core_copies = {}
    for i in order:
        there = lax.rem(chip + i, chips)
        core_copies[i] = send(
            part_ref.at[1 - core, there], core_in.at[i], core_send.at[i], core_recv.at[i], mate
        )
    plane_copies = {}
    for i in order:
        there = lax.rem(chip + i, chips)
        core_copies[i].wait_recv()
        plane_sum[i] = part_ref[core, there] + core_in[i]
        if i > 0:
            for j in band_order:
                band = lax.rem(lat + j, bands)
                plane_copies[i, j] = send(
                    plane_sum.at[i, band], plane_in.at[i - 1, j],
                    plane_send.at[i - 1, j], plane_recv.at[i - 1, j], plane[i - 1],
                )
    band_copies = {}
    for j in band_order:
        band = lax.rem(lat + j, bands)
        total = plane_sum[0, band]
        for i in range(1, chips):
            plane_copies[i, j].wait_recv()
            total = total + plane_in[i - 1, j]
        band_sum[j] = total
        if j > 0:
            band_copies[j] = send(
                band_sum.at[j], band_in.at[j - 1], band_send.at[j - 1], band_recv.at[j - 1],
                column[j - 1],
            )
    total = band_sum[0]
    for j in range(1, bands):
        band_copies[j].wait_recv()
        total = total + band_in[j - 1]
    final[...] = total
    last = send(final, other, last_send, last_recv, mate)
    out_ref[core] = total
    last.wait_recv()
    out_ref[1 - core] = other[...]
    for copy in [*core_copies.values(), *plane_copies.values(), *band_copies.values(), last]:
        copy.wait_send()


def shards(fields, weights, pair_slots, pair_counts, requests, eofs):
    lat_count, lon_count = lax.axis_size("lat"), lax.axis_size("lon")
    lat_index, lon_index = lax.axis_index("lat"), lax.axis_index("lon")
    device = lat_index * lon_count + lon_index
    grids, src_tiles, cells, columns = fields.shape
    tiles, pairs = weights.shape[1], weights.shape[2]
    modes = eofs.shape[0]
    asked = requests.shape[2]
    up = [(i, (i + 1) % lon_count) for i in range(lon_count)]
    down = [(j, i) for i, j in up]
    before = lax.ppermute(fields, "lon", up)
    after = lax.ppermute(fields, "lon", down)

    wanted = lax.dynamic_index_in_dim(requests, device, 1, keepdims=False).reshape(-1)
    sector = wanted // src_tiles - lat_index * lon_count
    relative = (sector - lon_index + 1 + lon_count) % lon_count
    local_tiles = wanted % src_tiles
    live = jnp.arange(pairs, dtype=jnp.int32) < pair_counts[:, :, None]
    slots = jnp.where(live, pair_slots, asked).reshape(-1)

    halves = 2
    width = halves * LANES
    block = 4
    while tiles % block:
        block //= 2
    basis = pl.pallas_call(
        functools.partial(basis_kernel, block, tiles),
        out_shape=jax.ShapeDtypeStruct((grids, asked * cells, 3 * width), jnp.bfloat16),
        grid_spec=pltpu.PrefetchScalarGridSpec(
            num_scalar_prefetch=1,
            grid=(tiles // block,),
            in_specs=[
                pl.BlockSpec((grids, block, pairs, cells, TT), lambda s, _: (0, s, 0, 0, 0)),
                pl.BlockSpec((modes, block * TT), lambda s, _: (0, s)),
            ],
            out_specs=pl.BlockSpec((grids, asked * cells, 3 * width), lambda s, _: (0, 0, 0)),
            scratch_shapes=[pltpu.VMEM(((asked + 1) * cells, width), jnp.float32)] * grids,
        ),
        cost_estimate=pl.CostEstimate(
            flops=2 * weights.size * modes, bytes_accessed=2 * (weights.size + eofs.size),
            transcendentals=0,
        ),
    )(slots, weights, eofs)

    chips = lon_count // 2
    rows = grids * columns // (lat_count * chips)
    smem = pl.BlockSpec(memory_space=pltpu.SMEM)
    vmem = pl.BlockSpec(memory_space=pltpu.VMEM)
    part = pl.pallas_call(
        project_kernel,
        out_shape=jax.ShapeDtypeStruct((halves, chips, lat_count, rows, LANES), jnp.float32),
        in_specs=[smem, smem, vmem, vmem, vmem, vmem],
        out_specs=vmem,
        scratch_shapes=[pltpu.VMEM((asked * cells, columns), jnp.bfloat16)],
    )(relative, local_tiles, before, fields, after, basis)

    dma = pltpu.SemaphoreType.DMA
    buffer = lambda *shape: pltpu.VMEM((*shape, rows, LANES), jnp.float32)
    summed = pl.pallas_call(
        reduce_kernel,
        out_shape=jax.ShapeDtypeStruct((halves, rows, LANES), jnp.float32),
        in_specs=[vmem],
        out_specs=vmem,
        scratch_shapes=[
            buffer(chips, lat_count), buffer(chips, lat_count), buffer(chips - 1, lat_count),
            buffer(lat_count), buffer(lat_count - 1), buffer(), buffer(),
            dma((chips,)), dma((chips,)),
            dma((chips - 1, lat_count)), dma((chips - 1, lat_count)),
            dma((lat_count - 1,)), dma((lat_count - 1,)),
            dma(()), dma(()),
        ],
        compiler_params=pltpu.CompilerParams(collective_id=0, has_side_effects=True),
    )(part)
    mine = lax.dynamic_slice_in_dim(summed, lax.rem(lon_index, 2) * (rows // 2), rows // 2, 1)
    joined = jnp.transpose(mine, (0, 2, 1)).reshape(width, rows // 2)
    return joined[:modes]


def solution(mesh):
    return jax.shard_map(
        shards,
        mesh=mesh,
        in_specs=(
            P(None, ("lat", "lon"), None, None),
            P(None, ("lat", "lon"), None, None, None),
            P(None, ("lat", "lon"), None),
            P(None, ("lat", "lon")),
            P(),
            P(None, ("lat", "lon")),
        ),
        out_specs=P(None, ("lat", "lon")),
        check_vma=False,
    )
```

profile of v0, /device:TPU:0, one launch (start us, length us, event | category | flops | bytes accessed | tf_op | source)
XLA Modules:
  0.0 57.6 jit_solution(1318703172472742034)
XLA Ops:
  0.0 0.0 copy-start
  0.0 0.5 collective-permute-start
  0.5 2.9 %collective-permute-start.1 = (bf16[3,16,32,384]{3,2,1,0:T(8,128)(2,1)}, bf16[3,16,32,384]{3,2,1,0:T(8,128)(2,1)S(1)}, u32[]{:S(2)}, u32[]{:S(2)}) collective-permute-start(bf16[3,16,32,384]{3,2,1,0:T(8,128)(2,1)} %own_ref.1), channel_id=1, source_target_pairs={{1,0},{2,1},{3,2},{4,3},{5,4},{6,5},{7,6},{0,7},{9,8},{10,9},{11,1... | collective-permute-start | bytes 3538952 | tf_op jit(solution)/shard_map/ppermute | solution.py:167
  3.4 0.0 copy-done
  3.4 0.2 dynamic-slice_reduce_fusion
  3.6 0.1 reshape.11
  3.7 0.7 %fusion = s32[3,32,8]{1,2,0:T(8,128)S(1)} fusion(s32[3,32,8]{1,2,0:T(8,128)} %param.8, s32[3,32]{1,0:T(4,128)} %param.9), kind=kLoop, calls=%fused_computation.4 | loop fusion | flops 1536 | bytes 6528 | tf_op jit(solution)/shard_map/jit(_where)/select_n | solution.py:174
  4.4 0.1 copy.7
  4.5 0.7 %reshape.12.slot_ref = s32[768]{0:T(1024)} reshape(s32[3,32,8]{2,1,0:T(8,128)S(1)} %copy.7) | data formatting | bytes 6144 | tf_op jit(solution)/shard_map/reshape | solution.py:174
  5.2 10.9 %shard_map.64.basis_ref = bf16[3,512,768]{2,1,0:T(8,128)(2,1)} custom-call(s32[768]{0:T(1024)} %reshape.12.slot_ref, bf16[3,32,8,32,128]{4,3,2,1,0:T(8,128)(2,1)} %weight_ref.1, bf16[200,4096]{1,0:T(8,128)(2,1)} %eof_ref.1), custom_call_target="tpu_custom_call" | custom-call | flops 1258291200 | bytes 7929856 | tf_op jit(solution)/shard_map/pallas_call | solution.py:181
  16.1 0.6 %and_select_fusion = (s32[48]{0:T(128)}, s32[48]{0:T(128)}) fusion(s32[48]{0:T(128)S(1)} %reshape.11, s32[]{:T(128)S(6)} %axis_index.25, s32[]{:T(128)S(6)} %mul.7), kind=kLoop, calls=%fused_computation.7 | loop fusion | flops 1584 | bytes 584 | tf_op jit(solution)/shard_map/jit(remainder)/select_n | solution.py:172
  16.7 10.8 %collective-permute-done.before_ref = bf16[3,16,32,384]{3,2,1,0:T(8,128)(2,1)S(1)} collective-permute-done((bf16[3,16,32,384]{3,2,1,0:T(8,128)(2,1)}, bf16[3,16,32,384]{3,2,1,0:T(8,128)(2,1)S(1)}, u32[]{:S(2)}, u32[]{:S(2)}) %collective-permute-start) | collective-permute-done | bytes 1179680 | tf_op jit(solution)/shard_map/ppermute | solution.py:166
  27.5 0.0 copy-start.1
  27.5 1.6 %collective-permute-done.1.after_ref = bf16[3,16,32,384]{3,2,1,0:T(8,128)(2,1)S(1)} collective-permute-done((bf16[3,16,32,384]{3,2,1,0:T(8,128)(2,1)}, bf16[3,16,32,384]{3,2,1,0:T(8,128)(2,1)S(1)}, u32[]{:S(2)}, u32[]{:S(2)}) %collective-permute-start.1) | collective-permute-done | bytes 1179680 | tf_op jit(solution)/shard_map/ppermute | solution.py:167
  29.1 0.0 copy-start.2
  29.1 0.0 copy-done.1
  29.1 1.0 %copy-done.2 = bf16[3,16,32,384]{3,2,1,0:T(8,128)(2,1)} copy-done((bf16[3,16,32,384]{3,2,1,0:T(8,128)(2,1)}, bf16[3,16,32,384]{3,2,1,0:T(8,128)(2,1)S(1)}, u32[]{:S(2)}) %copy-start.2) | copy-done | bytes 1179672
  30.1 5.3 %shard_map.65.part_ref = f32[2,4,4,72,128]{4,3,2,1,0:T(8,128)} custom-call(s32[48]{0:T(128)} %get-tuple-element.6.rel_ref, s32[48]{0:T(128)} %get-tuple-element.5.tile_ref, bf16[3,16,32,384]{3,2,1,0:T(8,128)(2,1)} %copy-done.1, bf16[3,16,32,384]{3,2,1,0:T(8,128)(2,1)} %own_ref.1, bf16[3,16,32,384]{3,2,1,0:T(8,128)(2,1)} %copy-done.2, ...), custom_call_target="tpu_custom_call" | custom-call | tf_op jit(solution)/shard_map/pallas_call | solution.py:204
  35.4 20.7 %shard_map.66 = f32[2,72,128]{2,1,0:T(8,128)} custom-call(f32[2,4,4,72,128]{4,3,2,1,0:T(8,128)} %shard_map.65.part_ref), custom_call_target="tpu_custom_call" | custom-call | tf_op jit(solution)/shard_map/pallas_call | solution.py:214
  56.1 0.8 %dynamic-slice_bitcast_fusion = f32[2,128,36]{1,2,0:T(8,128)S(1)} fusion(f32[2,72,128]{2,1,0:T(8,128)} %shard_map.66, s32[]{:T(128)S(6)} %select_n.32), kind=kLoop, calls=%fused_computation | loop fusion | bytes 73732 | tf_op jit(solution)/shard_map/transpose | solution.py:230
  57.0 0.6 %copy.9 = f32[5,8,2,128]{3,1,2,0:T(8,128)} copy(f32[5,8,2,128]{3,2,1,0:T(2,128)S(1)} %bitcast.10) | data formatting | bytes 81920
  (2 shorter events, 0.0 us)
Async XLA Ops:
  0.0 3.4 %copy-start = (s32[3,32,16]{1,2,0:T(8,128)S(1)}, s32[3,32,16]{1,2,0:T(8,128)}, u32[]{:S(2)}) copy-start(s32[3,32,16]{1,2,0:T(8,128)} %param.10) | copy-start | bytes 18436
  0.0 27.5 %collective-permute-start = (bf16[3,16,32,384]{3,2,1,0:T(8,128)(2,1)}, bf16[3,16,32,384]{3,2,1,0:T(8,128)(2,1)S(1)}, u32[]{:S(2)}, u32[]{:S(2)}) collective-permute-start(bf16[3,16,32,384]{3,2,1,0:T(8,128)(2,1)} %own_ref.1), channel_id=1, source_target_pairs={{0,1},{1,2},{2,3},{3,4},{4,5},{5,6},{6,7},{7,0},{8,9},{9,10},{10,1... | collective-permute-start | bytes 3538952 | tf_op jit(solution)/shard_map/ppermute | solution.py:166
  0.5 28.6 %collective-permute-start.1 = (bf16[3,16,32,384]{3,2,1,0:T(8,128)(2,1)}, bf16[3,16,32,384]{3,2,1,0:T(8,128)(2,1)S(1)}, u32[]{:S(2)}, u32[]{:S(2)}) collective-permute-start(bf16[3,16,32,384]{3,2,1,0:T(8,128)(2,1)} %own_ref.1), channel_id=1, source_target_pairs={{1,0},{2,1},{3,2},{4,3},{5,4},{6,5},{7,6},{0,7},{9,8},{10,9},{11,1... | collective-permute-start | bytes 3538952 | tf_op jit(solution)/shard_map/ppermute | solution.py:167
  27.5 1.6 %copy-start.1 = (bf16[3,16,32,384]{3,2,1,0:T(8,128)(2,1)}, bf16[3,16,32,384]{3,2,1,0:T(8,128)(2,1)S(1)}, u32[]{:S(2)}) copy-start(bf16[3,16,32,384]{3,2,1,0:T(8,128)(2,1)S(1)} %collective-permute-done.before_ref) | copy-start | bytes 3538948
  29.1 1.1 %copy-start.2 = (bf16[3,16,32,384]{3,2,1,0:T(8,128)(2,1)}, bf16[3,16,32,384]{3,2,1,0:T(8,128)(2,1)S(1)}, u32[]{:S(2)}) copy-start(bf16[3,16,32,384]{3,2,1,0:T(8,128)(2,1)S(1)} %collective-permute-done.1.after_ref) | copy-start | bytes 3538948
where the time goes:
time: 58 us; the launch traced here: 57.6 us
  Pallas kernels  36.9 us (64%)
  waiting for transfers between devices  12.3 us (21%)
  local copies, waits for them, and re-layouts  3.6 us (6%)
  starting transfers between devices  3.42 us (6%)
  other arithmetic  1.33 us (2%)
    pallas_call x1, Pallas kernels, shards(): pl.pallas_call(reduce_kernel, out_shape=jax.ShapeDtypeStruct((halves, row...  20.7 us
    pallas_call x1, Pallas kernels, shards(): pl.pallas_call(functools.partial(basis_kernel, block, tiles), out_shape=j...  10.9 us
    ppermute x1, waiting for transfers between devices, shards(): before = lax.ppermute(fields, 'lon', up)  10.8 us
    pallas_call x1, Pallas kernels, shards(): pl.pallas_call(project_kernel, out_shape=jax.ShapeDtypeStruct((halves, ch...  5.25 us
    ppermute x1, starting transfers between devices, shards(): after = lax.ppermute(fields, 'lon', down)  2.93 us
    unnamed x8, local copies, waits for them, and re-layouts  1.7 us
    ppermute x1, waiting for transfers between devices, shards(): after = lax.ppermute(fields, 'lon', down)  1.57 us
  transfers between devices with their start and end apart: 2, of which 2 were waited for; matrix products, arithmetic and copies ran while one was open for 4% of the time, Pallas kernels for 19%

commit v1 on v0

--- a/solution.py
+++ b/solution.py
@@ -52,15 +52,37 @@
                 out_ref[g, :, i * width:(i + 1) * width] = term
 
 
-def project_kernel(rel_ref, tile_ref, before_ref, own_ref, after_ref, basis_ref, out_ref, source):
+def pack_kernel(request_ref, own_ref, up_ref, down_ref):
+    grids, src_tiles, _, _ = own_ref.shape
+    lon_count = lax.axis_size("lon")
+    lat, lon = lax.axis_index("lat"), lax.axis_index("lon")
+    first = (lat * lon_count + lon) * src_tiles
+    for target, shift in ((up_ref, 1), (down_ref, lon_count - 1)):
+        asker = lat * lon_count + lax.rem(lon + shift, lon_count)
+        for g in range(grids):
+            def place(q, count, g=g, target=target, asker=asker):
+                tile = request_ref[g, q, asker] - first
+                held = jnp.logical_and(tile >= 0, tile < src_tiles)
+
+                @pl.when(held)
+                def _():
+                    target[g, count] = own_ref[g, tile]
+
+                return count + held.astype(jnp.int32)
+
+            lax.fori_loop(0, request_ref.shape[1], place, jnp.int32(0), unroll=True)
+
+
+def project(rel_ref, near_ref, tile_ref, before_ref, own_ref, after_ref, basis_ref, part, source):
     grids, _, cells, columns = own_ref.shape
-    _, chips, bands, rows, _ = out_ref.shape
+    _, chips, bands, rows, _ = part.shape
     wanted = rel_ref.shape[0] // grids
     width = basis_ref.shape[2] // 3
     for g in range(grids):
         for j in range(wanted):
-            rel, tile = rel_ref[g * wanted + j], tile_ref[g * wanted + j]
-            side = jnp.where(rel == 0, before_ref[g, tile], after_ref[g, tile])
+            k = g * wanted + j
+            rel, near, tile = rel_ref[k], near_ref[k], tile_ref[k]
+            side = jnp.where(rel == 0, before_ref[g, near], after_ref[g, near])
             source[j * cells:(j + 1) * cells] = jnp.where(rel == 1, own_ref[g, tile], side)
         product = lax.dot_general(
             source[...], basis_ref[g], (((0,), (0,)), ((), ())),
@@ -74,19 +96,20 @@
         for chunk in range(chips * bands):
             low = max(chunk * rows, first)
             high = min((chunk + 1) * rows, first + columns)
-            for half in range(out_ref.shape[0]):
+            for half in range(part.shape[0]):
                 if low < high:
-                    out_ref[
+                    part[
                         half, chunk % chips, chunk // chips,
                         low - chunk * rows:high - chunk * rows, :,
                     ] = total[low - first:high - first, half * LANES:(half + 1) * LANES]
 
 
 def reduce_kernel(
-    part_ref, out_ref, core_in, plane_sum, plane_in, band_sum, band_in, final, other,
+    rel_ref, near_ref, tile_ref, before_ref, own_ref, after_ref, basis_ref, out_ref,
+    source, part, core_in, plane_sum, plane_in, band_sum, band_in, final, other,
     core_send, core_recv, plane_send, plane_recv, band_send, band_recv, last_send, last_recv,
 ):
-    _, chips, bands, _, _ = part_ref.shape
+    _, chips, bands, _, _ = part.shape
     lat, lon = lax.axis_index("lat"), lax.axis_index("lon")
     core, chip = lax.rem(lon, 2), lon // 2
     mate = (lat, chip * 2 + 1 - core)
@@ -96,6 +119,9 @@
     partners = [mate] + plane + column
     for partner in partners:
         pl.semaphore_signal(barrier, inc=1, device_id=partner, device_id_type=MESH)
+    project(
+        rel_ref, near_ref, tile_ref, before_ref, own_ref, after_ref, basis_ref, part, source
+    )
     pl.semaphore_wait(barrier, len(partners))
 
     order = list(range(1, chips)) + [0]
@@ -109,47 +135,49 @@
         copy.start()
         return copy
 
-    core_copies = {}
-    for i in order:
-        there = lax.rem(chip + i, chips)
-        core_copies[i] = send(
-            part_ref.at[1 - core, there], core_in.at[i], core_send.at[i], core_recv.at[i], mate
-        )
-    plane_copies = {}
-    for i in order:
-        there = lax.rem(chip + i, chips)
-        core_copies[i].wait_recv()
-        plane_sum[i] = part_ref[core, there] + core_in[i]
-        if i > 0:
-            for j in band_order:
-                band = lax.rem(lat + j, bands)
-                plane_copies[i, j] = send(
-                    plane_sum.at[i, band], plane_in.at[i - 1, j],
+    copies, arrivals = [], {}
+    for j in band_order:
+        for i in order:
+            there, band = lax.rem(chip + i, chips), lax.rem(lat + j, bands)
+            arrivals["core", i, j] = send(
+                part.at[1 - core, there, band], core_in.at[i, j],
+                core_send.at[i, j], core_recv.at[i, j], mate,
+            )
+    for j in band_order:
+        for i in order:
+            there, band = lax.rem(chip + i, chips), lax.rem(lat + j, bands)
+            arrivals["core", i, j].wait_recv()
+            plane_sum[i, j] = part[core, there, band] + core_in[i, j]
+            if i > 0:
+                arrivals["plane", i, j] = send(
+                    plane_sum.at[i, j], plane_in.at[i - 1, j],
                     plane_send.at[i - 1, j], plane_recv.at[i - 1, j], plane[i - 1],
                 )
-    band_copies = {}
     for j in band_order:
-        band = lax.rem(lat + j, bands)
-        total = plane_sum[0, band]
+        total = plane_sum[0, j]
         for i in range(1, chips):
-            plane_copies[i, j].wait_recv()
+            arrivals["plane", i, j].wait_recv()
             total = total + plane_in[i - 1, j]
         band_sum[j] = total
         if j > 0:
-            band_copies[j] = send(
+            arrivals["band", j] = send(
                 band_sum.at[j], band_in.at[j - 1], band_send.at[j - 1], band_recv.at[j - 1],
                 column[j - 1],
             )
     total = band_sum[0]
     for j in range(1, bands):
-        band_copies[j].wait_recv()
+        arrivals["band", j].wait_recv()
         total = total + band_in[j - 1]
     final[...] = total
-    last = send(final, other, last_send, last_recv, mate)
-    out_ref[core] = total
-    last.wait_recv()
-    out_ref[1 - core] = other[...]
-    for copy in [*core_copies.values(), *plane_copies.values(), *band_copies.values(), last]:
+    arrivals["last"] = send(final, other, last_send, last_recv, mate)
+    arrivals["last"].wait_recv()
+    theirs = other[...]
+    left = jnp.where(core == 0, total, theirs)
+    right = jnp.where(core == 0, theirs, total)
+    joined = jnp.concatenate([left, right], axis=1)
+    height, modes = out_ref.shape
+    out_ref[...] = jnp.where(core == 0, joined[:height], joined[height:])[:, :modes]
+    for copy in arrivals.values():
         copy.wait_send()
 
 
@@ -163,13 +191,24 @@
     asked = requests.shape[2]
     up = [(i, (i + 1) % lon_count) for i in range(lon_count)]
     down = [(j, i) for i, j in up]
-    before = lax.ppermute(fields, "lon", up)
-    after = lax.ppermute(fields, "lon", down)
-
-    wanted = lax.dynamic_index_in_dim(requests, device, 1, keepdims=False).reshape(-1)
+    smem = pl.BlockSpec(memory_space=pltpu.SMEM)
+    vmem = pl.BlockSpec(memory_space=pltpu.VMEM)
+    packed = jax.ShapeDtypeStruct((grids, asked // 2, cells, columns), fields.dtype)
+    upward, downward = pl.pallas_call(
+        pack_kernel, out_shape=[packed, packed], in_specs=[smem, vmem], out_specs=[vmem, vmem],
+    )(jnp.transpose(requests, (0, 2, 1)), fields)
+    before = lax.ppermute(upward, "lon", up)
+    after = lax.ppermute(downward, "lon", down)
+
+    wanted = lax.dynamic_index_in_dim(requests, device, 1, keepdims=False)
     sector = wanted // src_tiles - lat_index * lon_count
     relative = (sector - lon_index + 1 + lon_count) % lon_count
-    local_tiles = wanted % src_tiles
+    earlier = jnp.arange(asked)[None, :] < jnp.arange(asked)[:, None]
+    same = (relative[:, :, None] == relative[:, None, :]) & earlier
+    rank = jnp.sum(same, axis=2, dtype=jnp.int32)
+    near = jnp.where(relative == 1, 0, rank).reshape(-1)
+    local_tiles = jnp.where(relative == 1, wanted % src_tiles, 0).reshape(-1)
+    relative = relative.reshape(-1)
     live = jnp.arange(pairs, dtype=jnp.int32) < pair_counts[:, :, None]
     slots = jnp.where(live, pair_slots, asked).reshape(-1)
 
@@ -199,36 +238,26 @@
 
     chips = lon_count // 2
     rows = grids * columns // (lat_count * chips)
-    smem = pl.BlockSpec(memory_space=pltpu.SMEM)
-    vmem = pl.BlockSpec(memory_space=pltpu.VMEM)
-    part = pl.pallas_call(
-        project_kernel,
-        out_shape=jax.ShapeDtypeStruct((halves, chips, lat_count, rows, LANES), jnp.float32),
-        in_specs=[smem, smem, vmem, vmem, vmem, vmem],
-        out_specs=vmem,
-        scratch_shapes=[pltpu.VMEM((asked * cells, columns), jnp.bfloat16)],
-    )(relative, local_tiles, before, fields, after, basis)
-
     dma = pltpu.SemaphoreType.DMA
     buffer = lambda *shape: pltpu.VMEM((*shape, rows, LANES), jnp.float32)
     summed = pl.pallas_call(
         reduce_kernel,
-        out_shape=jax.ShapeDtypeStruct((halves, rows, LANES), jnp.float32),
-        in_specs=[vmem],
+        out_shape=jax.ShapeDtypeStruct((rows // 2, modes), jnp.float32),
+        in_specs=[smem, smem, smem, vmem, vmem, vmem, vmem],
         out_specs=vmem,
         scratch_shapes=[
+            pltpu.VMEM((asked * cells, columns), jnp.bfloat16),
+            buffer(halves, chips, lat_count),
             buffer(chips, lat_count), buffer(chips, lat_count), buffer(chips - 1, lat_count),
             buffer(lat_count), buffer(lat_count - 1), buffer(), buffer(),
-            dma((chips,)), dma((chips,)),
+            dma((chips, lat_count)), dma((chips, lat_count)),
             dma((chips - 1, lat_count)), dma((chips - 1, lat_count)),
             dma((lat_count - 1,)), dma((lat_count - 1,)),
             dma(()), dma(()),
         ],
         compiler_params=pltpu.CompilerParams(collective_id=0, has_side_effects=True),
-    )(part)
-    mine = lax.dynamic_slice_in_dim(summed, lax.rem(lon_index, 2) * (rows // 2), rows // 2, 1)
-    joined = jnp.transpose(mine, (0, 2, 1)).reshape(width, rows // 2)
-    return joined[:modes]
+    )(relative, near, local_tiles, before, fields, after, basis)
+    return jnp.transpose(summed)
 
 
 def solution(mesh):

time: 58 us -> 44.2 us (0.76)
  waiting for transfers between devices: 12.3 us -> 0.01 us
  Pallas kernels: 36.9 us -> 33.9 us
  other arithmetic: 1.33 us -> 3.01 us
    ppermute x2, waiting for transfers between devices: 12.3 us -> 0.01 us  [the longest x1 0.01 us: shards(): before = lax.ppermute(upward, 'lon', up)]
    pallas_call x2, Pallas kernels: 26 us -> 23.1 us  [the longest x1 19.6 us: shards(): pl.pallas_call(reduce_kernel, out_shape=jax.ShapeDtypeStruct((rows // 2,...]
    select_n x1 -> x4, other arithmetic: 0.61 us -> 2.08 us  [the longest x2 1.02 us: shards(): relative = (sector - lon_index + 1 + lon_count) % lon_count]
    transpose x2 -> x0, local copies, waits for them, and re-layouts: 0.84 us -> none  [shards(): joined = jnp.transpose(mine, (0, 2, 1)).reshape(width, rows // 2)]
    unnamed x8 -> x7, local copies, waits for them, and re-layouts: 1.7 us -> 2.4 us
  transfers between devices with their start and end apart: 2 -> 2, of which waited for: 2 -> 0; matrix products, arithmetic and copies ran while one was open for 4% -> 9% of each run, Pallas kernels for 19% -> 25%
where the time goes in v1:
time: 44.2 us; the launch traced here: 43.7 us
  Pallas kernels  33.9 us (77%)
  starting transfers between devices  3.35 us (8%)
  local copies, waits for them, and re-layouts  3.33 us (8%)
  other arithmetic  3.01 us (7%)
    pallas_call x1, Pallas kernels, shards(): pl.pallas_call(reduce_kernel, out_shape=jax.ShapeDtypeStruct((rows // 2,...  19.6 us
    pallas_call x1, Pallas kernels, shards(): pl.pallas_call(functools.partial(basis_kernel, block, tiles), out_shape=j...  10.8 us
    pallas_call x1, Pallas kernels, shards(): pl.pallas_call(pack_kernel, out_shape=[packed, packed], in_specs=[smem, v...  3.56 us
    ppermute x1, starting transfers between devices, shards(): after = lax.ppermute(downward, 'lon', down)  2.87 us
    unnamed x7, local copies, waits for them, and re-layouts  2.4 us
    select_n x2, other arithmetic, shards(): relative = (sector - lon_index + 1 + lon_count) % lon_count  1.02 us
  transfers between devices with their start and end apart: 2, of which 0 were waited for; matrix products, arithmetic and copies ran while one was open for 9% of the time, Pallas kernels for 25%

profile of v1, /device:TPU:0, one launch (start us, length us, event | category | flops | bytes accessed | tf_op | source)
XLA Modules:
  0.0 43.7 jit_solution(12606829627459363171)
XLA Ops:
  0.0 3.6 %shard_map.64 = (bf16[3,8,32,384]{3,2,1,0:T(8,128)(2,1)}, bf16[3,8,32,384]{3,2,1,0:T(8,128)(2,1)}) custom-call(s32[3,16,32]{2,1,0:T(8,128)} %bitcast.3, bf16[3,16,32,384]{3,2,1,0:T(8,128)(2,1)} %own_ref.3), custom_call_target="tpu_custom_call" | custom-call | tf_op jit(solution)/shard_map/pallas_call | solution.py:197
  3.6 0.5 %collective-permute-start = (bf16[3,8,32,384]{3,2,1,0:T(8,128)(2,1)}, bf16[3,8,32,384]{3,2,1,0:T(8,128)(2,1)S(1)}, u32[]{:S(2)}, u32[]{:S(2)}) collective-permute-start(bf16[3,8,32,384]{3,2,1,0:T(8,128)(2,1)} %get-tuple-element.7), channel_id=1, source_target_pairs={{0,1},{1,2},{2,3},{3,4},{4,5},{5,6},{6,7},{7,0},{8,9},{9,10},{10,1... | collective-permute-start | bytes 1769480 | tf_op jit(solution)/shard_map/ppermute | solution.py:200
  4.0 2.9 %collective-permute-start.1 = (bf16[3,8,32,384]{3,2,1,0:T(8,128)(2,1)}, bf16[3,8,32,384]{3,2,1,0:T(8,128)(2,1)S(1)}, u32[]{:S(2)}, u32[]{:S(2)}) collective-permute-start(bf16[3,8,32,384]{3,2,1,0:T(8,128)(2,1)} %get-tuple-element.8), channel_id=1, source_target_pairs={{1,0},{2,1},{3,2},{4,3},{5,4},{6,5},{7,6},{0,7},{9,8},{10,9},{11,1... | collective-permute-start | bytes 1769480 | tf_op jit(solution)/shard_map/ppermute | solution.py:201
  6.9 1.0 %fusion.5 = (s32[3,16]{1,0:T(4,128)S(1)}, s32[3,16]{1,0:T(4,128)S(1)}) fusion(s32[3,32,16]{1,2,0:T(8,128)} %param.10, s32[]{:T(128)S(6)} %select_n.59, s32[]{:T(128)S(6)} %axis_index.25, s32[]{:T(128)S(6)} %mul.4), kind=kLoop, calls=%fused_computation.12 | loop fusion | flops 1392 | bytes 588 | tf_op jit(solution)/shard_map/jit(remainder)/select_n | solution.py:205
  7.9 0.7 %fusion.7 = s32[3,32,8]{1,2,0:T(8,128)S(1)} fusion(s32[3,32,8]{1,2,0:T(8,128)} %param.8, s32[3,32]{1,0:T(4,128)} %param.9), kind=kLoop, calls=%fused_computation.18 | loop fusion | flops 1536 | bytes 6528 | tf_op jit(solution)/shard_map/jit(_where)/select_n | solution.py:213
  8.7 0.2 convert_reduce_fusion
  8.9 0.1 squeeze.6
  9.0 0.1 reduce_sum.12
  9.0 0.1 copy.8
  9.1 0.7 %reshape.65.slot_ref = s32[768]{0:T(1024)} reshape(s32[3,32,8]{2,1,0:T(8,128)S(1)} %copy.8) | data formatting | bytes 6144 | tf_op jit(solution)/shard_map/reshape | solution.py:213
  9.8 10.8 %shard_map.65.basis_ref = bf16[3,512,768]{2,1,0:T(8,128)(2,1)} custom-call(s32[768]{0:T(1024)} %reshape.65.slot_ref, bf16[3,32,8,32,128]{4,3,2,1,0:T(8,128)(2,1)} %weight_ref.1, bf16[200,4096]{1,0:T(8,128)(2,1)} %eof_ref.1), custom_call_target="tpu_custom_call" | custom-call | flops 1258291200 | bytes 7929856 | tf_op jit(solution)/shard_map/pallas_call | solution.py:220
  20.6 0.5 %compare_select_fusion.5 = (s32[48]{0:T(128)}, s32[48]{0:T(128)S(1)}) fusion(s32[48]{0:T(128)S(1)} %squeeze.6, s32[]{:T(128)S(6)} %axis_index.25, s32[]{:T(128)S(6)} %mul.4), kind=kLoop, calls=%fused_computation.42 | loop fusion | flops 1680 | bytes 584 | tf_op jit(solution)/shard_map/jit(_where)/select_n | solution.py:210
  21.2 0.0 copy-start.2
  21.2 0.5 %compare_select_fusion.6.near_ref = s32[48]{0:T(128)} fusion(s32[48]{0:T(128)S(1)} %reduce_sum.12, s32[48]{0:T(128)S(1)} %get-tuple-element.12.rel_ref), kind=kLoop, calls=%fused_computation.43 | loop fusion | flops 96 | bytes 576 | tf_op jit(solution)/shard_map/jit(_where)/select_n | solution.py:209
  21.7 0.0 collective-permute-done.before_ref
  21.7 0.0 copy-start
  21.7 0.0 collective-permute-done.1.after_ref
  21.7 0.0 copy-start.1
  21.7 0.0 copy-done.2
  21.7 0.8 %copy-done = bf16[3,8,32,384]{3,2,1,0:T(8,128)(2,1)} copy-done((bf16[3,8,32,384]{3,2,1,0:T(8,128)(2,1)}, bf16[3,8,32,384]{3,2,1,0:T(8,128)(2,1)S(1)}, u32[]{:S(2)}) %copy-start) | copy-done | bytes 589848
  22.5 0.2 copy-done.1
  22.7 19.6 %shard_map.66 = f32[36,200]{1,0:T(8,128)} custom-call(s32[48]{0:T(128)} %copy-done.2, s32[48]{0:T(128)} %compare_select_fusion.6.near_ref, s32[48]{0:T(128)} %get-tuple-element.11.tile_ref, bf16[3,8,32,384]{3,2,1,0:T(8,128)(2,1)} %copy-done, bf16[3,16,32,384]{3,2,1,0:T(8,128)(2,1)} %own_ref.3, bf16[3,8,32,384]{3,2,1,0:T(8,128)(2,1)} %copy-done.1, ...), custom_call_target="tpu_custom_call" | custom-call | tf_op jit(solution)/shard_map/pallas_call | solution.py:243
  42.3 1.4 %copy.10 = f32[200,36]{0,1:T(8,128)} copy(f32[200,36]{0,1:T(8,128)} %bitcast.2) | data formatting | bytes 57600
  (2 shorter events, 0.0 us)
Async XLA Ops:
  3.6 18.2 %collective-permute-start = (bf16[3,8,32,384]{3,2,1,0:T(8,128)(2,1)}, bf16[3,8,32,384]{3,2,1,0:T(8,128)(2,1)S(1)}, u32[]{:S(2)}, u32[]{:S(2)}) collective-permute-start(bf16[3,8,32,384]{3,2,1,0:T(8,128)(2,1)} %get-tuple-element.7), channel_id=1, source_target_pairs={{0,1},{1,2},{2,3},{3,4},{4,5},{5,6},{6,7},{7,0},{8,9},{9,10},{10,1... | collective-permute-start | bytes 1769480 | tf_op jit(solution)/shard_map/ppermute | solution.py:200
  4.0 17.7 %collective-permute-start.1 = (bf16[3,8,32,384]{3,2,1,0:T(8,128)(2,1)}, bf16[3,8,32,384]{3,2,1,0:T(8,128)(2,1)S(1)}, u32[]{:S(2)}, u32[]{:S(2)}) collective-permute-start(bf16[3,8,32,384]{3,2,1,0:T(8,128)(2,1)} %get-tuple-element.8), channel_id=1, source_target_pairs={{1,0},{2,1},{3,2},{4,3},{5,4},{6,5},{7,6},{0,7},{9,8},{10,9},{11,1... | collective-permute-start | bytes 1769480 | tf_op jit(solution)/shard_map/ppermute | solution.py:201
  21.2 0.6 %copy-start.2 = (s32[48]{0:T(128)}, s32[48]{0:T(128)S(1)}, u32[]{:S(2)}) copy-start(s32[48]{0:T(128)S(1)} %get-tuple-element.12.rel_ref) | copy-start | bytes 580
  21.7 0.8 %copy-start = (bf16[3,8,32,384]{3,2,1,0:T(8,128)(2,1)}, bf16[3,8,32,384]{3,2,1,0:T(8,128)(2,1)S(1)}, u32[]{:S(2)}) copy-start(bf16[3,8,32,384]{3,2,1,0:T(8,128)(2,1)S(1)} %collective-permute-done.before_ref) | copy-start | bytes 1769476
  21.7 1.0 %copy-start.1 = (bf16[3,8,32,384]{3,2,1,0:T(8,128)(2,1)}, bf16[3,8,32,384]{3,2,1,0:T(8,128)(2,1)S(1)}, u32[]{:S(2)}) copy-start(bf16[3,8,32,384]{3,2,1,0:T(8,128)(2,1)S(1)} %collective-permute-done.1.after_ref) | copy-start | bytes 1769476

commit v2 on v1

--- a/solution.py
+++ b/solution.py
@@ -11,6 +11,7 @@
 MONTHS = 24
 LANES = 128
 MESH = pl.DeviceIdType.MESH
+VMEM_LIMIT = 20 << 20
 
 
 def split_terms(value):
@@ -196,6 +197,7 @@
     packed = jax.ShapeDtypeStruct((grids, asked // 2, cells, columns), fields.dtype)
     upward, downward = pl.pallas_call(
         pack_kernel, out_shape=[packed, packed], in_specs=[smem, vmem], out_specs=[vmem, vmem],
+        compiler_params=pltpu.CompilerParams(vmem_limit_bytes=VMEM_LIMIT),
     )(jnp.transpose(requests, (0, 2, 1)), fields)
     before = lax.ppermute(upward, "lon", up)
     after = lax.ppermute(downward, "lon", down)
@@ -230,6 +232,7 @@
             out_specs=pl.BlockSpec((grids, asked * cells, 3 * width), lambda s, _: (0, 0, 0)),
             scratch_shapes=[pltpu.VMEM(((asked + 1) * cells, width), jnp.float32)] * grids,
         ),
+        compiler_params=pltpu.CompilerParams(vmem_limit_bytes=VMEM_LIMIT),
         cost_estimate=pl.CostEstimate(
             flops=2 * weights.size * modes, bytes_accessed=2 * (weights.size + eofs.size),
             transcendentals=0,
@@ -255,7 +258,9 @@
             dma((lat_count - 1,)), dma((lat_count - 1,)),
             dma(()), dma(()),
         ],
-        compiler_params=pltpu.CompilerParams(collective_id=0, has_side_effects=True),
+        compiler_params=pltpu.CompilerParams(
+            collective_id=0, has_side_effects=True, vmem_limit_bytes=VMEM_LIMIT
+        ),
     )(relative, near, local_tiles, before, fields, after, basis)
     return jnp.transpose(summed)
 

time: 44.2 us -> 39.4 us (0.89)
  Pallas kernels: 33.9 us -> 26.3 us
  local copies, waits for them, and re-layouts: 3.33 us -> 7.18 us
  other arithmetic: 3.01 us -> 1.98 us
    unnamed x7 -> x11, local copies, waits for them, and re-layouts: 2.4 us -> 6.84 us
    pallas_call x1, Pallas kernels: 10.8 us -> 7.02 us  [shards(): pl.pallas_call(functools.partial(basis_kernel, block, tiles), out_shape=j...]
    pallas_call x1, Pallas kernels: 19.6 us -> 17 us  [shards(): pl.pallas_call(reduce_kernel, out_shape=jax.ShapeDtypeStruct((rows // 2,...]
    pallas_call x1, Pallas kernels: 3.56 us -> 2.23 us  [shards(): pl.pallas_call(pack_kernel, out_shape=[packed, packed], in_specs=[smem, v...]
    reshape x1, local copies, waits for them, and re-layouts: 0.7 us -> 0.1 us  [shards(): slots = jnp.where(live, pair_slots, asked).reshape(-1)]
    select_n x1, other arithmetic: 0.53 us -> 0.01 us  [shards(): near = jnp.where(relative == 1, 0, rank).reshape(-1)]
    select_n x1, other arithmetic: 0.53 us -> 0.02 us  [shards(): local_tiles = jnp.where(relative == 1, wanted % src_tiles, 0).reshape(-1)]
  transfers between devices with their start and end apart: 2 -> 2, of which waited for: 0 -> 0; matrix products, arithmetic and copies ran while one was open for 9% -> 6% of each run, Pallas kernels for 25% -> 18%
where the time goes in v2:
time: 39.4 us; the launch traced here: 39 us
  Pallas kernels  26.3 us (67%)
  local copies, waits for them, and re-layouts  7.18 us (18%)
  starting transfers between devices  3.48 us (9%)
  other arithmetic  1.98 us (5%)
    pallas_call x1, Pallas kernels, shards(): pl.pallas_call(reduce_kernel, out_shape=jax.ShapeDtypeStruct((rows // 2,...  17 us
    pallas_call x1, Pallas kernels, shards(): pl.pallas_call(functools.partial(basis_kernel, block, tiles), out_shape=j...  7.02 us
    unnamed x11, local copies, waits for them, and re-layouts  6.84 us
    ppermute x1, starting transfers between devices, shards(): after = lax.ppermute(downward, 'lon', down)  2.9 us
    pallas_call x1, Pallas kernels, shards(): pl.pallas_call(pack_kernel, out_shape=[packed, packed], in_specs=[smem, v...  2.23 us
    select_n x2, other arithmetic, shards(): relative = (sector - lon_index + 1 + lon_count) % lon_count  1.02 us
  transfers between devices with their start and end apart: 2, of which 0 were waited for; matrix products, arithmetic and copies ran while one was open for 6% of the time, Pallas kernels for 18%

profile of v2, /device:TPU:0, one launch (start us, length us, event | category | flops | bytes accessed | tf_op | source)
XLA Modules:
  0.0 39.0 jit_solution(18374123970348493267)
XLA Ops:
  0.0 0.0 copy-start.1
  0.0 1.3 %copy-done.1 = bf16[3,16,32,384]{3,2,1,0:T(8,128)(2,1)S(1)} copy-done((bf16[3,16,32,384]{3,2,1,0:T(8,128)(2,1)S(1)}, bf16[3,16,32,384]{3,2,1,0:T(8,128)(2,1)}, u32[]{:S(2)}) %copy-start.1) | copy-done | bytes 1179672
  1.3 0.0 copy-start.4
  1.3 0.7 %copy-done.4 = s32[3,32,16]{1,2,0:T(8,128)S(1)} copy-done((s32[3,32,16]{1,2,0:T(8,128)S(1)}, s32[3,32,16]{1,2,0:T(8,128)}, u32[]{:S(2)}) %copy-start.4) | copy-done | bytes 6168
  2.0 2.2 %shard_map.64 = (bf16[3,8,32,384]{3,2,1,0:T(8,128)(2,1)S(1)}, bf16[3,8,32,384]{3,2,1,0:T(8,128)(2,1)S(1)}) custom-call(s32[3,16,32]{2,1,0:T(8,128)S(1)} %bitcast.3, bf16[3,16,32,384]{3,2,1,0:T(8,128)(2,1)S(1)} %copy-done.1), custom_call_target="tpu_custom_call" | custom-call | tf_op jit(solution)/shard_map/pallas_call | solution.py:198
  4.2 0.6 %collective-permute-start = (bf16[3,8,32,384]{3,2,1,0:T(8,128)(2,1)S(1)}, bf16[3,8,32,384]{3,2,1,0:T(8,128)(2,1)S(1)}, u32[]{:S(2)}, u32[]{:S(2)}) collective-permute-start(bf16[3,8,32,384]{3,2,1,0:T(8,128)(2,1)S(1)} %get-tuple-element.7), channel_id=1, source_target_pairs={{0,1},{1,2},{2,3},{3,4},{4,5},{5,6},{6,7},{7,0},{8,9},{9,10},{10,1... | collective-permute-start | bytes 1769480 | tf_op jit(solution)/shard_map/ppermute | solution.py:202
  4.8 2.9 %collective-permute-start.1 = (bf16[3,8,32,384]{3,2,1,0:T(8,128)(2,1)S(1)}, bf16[3,8,32,384]{3,2,1,0:T(8,128)(2,1)S(1)}, u32[]{:S(2)}, u32[]{:S(2)}) collective-permute-start(bf16[3,8,32,384]{3,2,1,0:T(8,128)(2,1)S(1)} %get-tuple-element.8), channel_id=1, source_target_pairs={{1,0},{2,1},{3,2},{4,3},{5,4},{6,5},{7,6},{0,7},{9,8},{10,9},{11,1... | collective-permute-start | bytes 1769480 | tf_op jit(solution)/shard_map/ppermute | solution.py:203
  7.7 1.0 %fusion.5 = (s32[3,16]{1,0:T(4,128)S(1)}, s32[3,16]{1,0:T(4,128)S(1)}) fusion(s32[3,32,16]{1,2,0:T(8,128)} %param.10, s32[]{:T(128)S(6)} %select_n.59, s32[]{:T(128)S(6)} %axis_index.25, s32[]{:T(128)S(6)} %mul.4), kind=kLoop, calls=%fused_computation.12 | loop fusion | flops 1392 | bytes 588 | tf_op jit(solution)/shard_map/jit(remainder)/select_n | solution.py:207
  8.8 0.7 %fusion.7 = s32[3,32,8]{1,2,0:T(8,128)S(1)} fusion(s32[3,32,8]{1,2,0:T(8,128)} %param.8, s32[3,32]{1,0:T(4,128)} %param.9), kind=kLoop, calls=%fused_computation.18 | loop fusion | flops 1536 | bytes 6528 | tf_op jit(solution)/shard_map/jit(_where)/select_n | solution.py:215
  9.5 0.2 convert_reduce_fusion
  9.7 0.1 squeeze.6
  9.8 0.1 reduce_sum.12
  9.9 0.1 copy.8
  9.9 0.1 reshape.65.slot_ref
  10.0 0.0 copy-start
  10.1 2.8 %copy-done = bf16[3,32,8,32,128]{4,3,2,1,0:T(8,128)(2,1)S(1)} copy-done((bf16[3,32,8,32,128]{4,3,2,1,0:T(8,128)(2,1)S(1)}, bf16[3,32,8,32,128]{4,3,2,1,0:T(8,128)(2,1)}, u32[]{:S(2)}) %copy-start) | copy-done | bytes 6291480
  12.8 0.0 copy-start.3
  12.8 1.4 %copy-done.3 = bf16[200,4096]{1,0:T(8,128)(2,1)S(1)} copy-done((bf16[200,4096]{1,0:T(8,128)(2,1)S(1)}, bf16[200,4096]{1,0:T(8,128)(2,1)}, u32[]{:S(2)}) %copy-start.3) | copy-done | bytes 1638424
  14.3 0.0 copy-start.2
  14.3 7.0 %shard_map.65.basis_ref = bf16[3,512,768]{2,1,0:T(8,128)(2,1)S(1)} custom-call(s32[768]{0:T(1024)S(1)} %reshape.65.slot_ref, bf16[3,32,8,32,128]{4,3,2,1,0:T(8,128)(2,1)S(1)} %copy-done, bf16[200,4096]{1,0:T(8,128)(2,1)S(1)} %copy-done.3), custom_call_target="tpu_custom_call" | custom-call | flops 1258291200 | bytes 7929856 | tf_op jit(solution)/shard_map/pallas_call | solution.py:222
  21.3 0.0 collective-permute-done.before_ref
  21.3 0.0 collective-permute-done.1.after_ref
  21.3 0.0 copy-done.2
  21.4 17.0 %shard_map.66 = f32[36,200]{1,0:T(8,128)S(1)} custom-call(s32[48]{0:T(128)S(1)} %get-tuple-element.12.rel_ref, s32[48]{0:T(128)S(1)} %compare_select_fusion.6.near_ref, s32[48]{0:T(128)S(1)} %get-tuple-element.11.tile_ref, bf16[3,8,32,384]{3,2,1,0:T(8,128)(2,1)S(1)} %collective-permute-done.before_ref, bf16[3,16,32,384]{3,2,1,0:T(8,128)(2,1)S(1)} %copy-done.2, ...), custom_call_target="tpu_custom_call" | custom-call | tf_op jit(solution)/shard_map/pallas_call | solution.py:246
  38.4 0.6 %copy.10 = f32[200,36]{0,1:T(8,128)} copy(f32[200,36]{0,1:T(8,128)S(1)} %bitcast.2) | data formatting | bytes 57600
  (4 shorter events, 0.1 us)
Async XLA Ops:
  0.0 1.3 %copy-start.1 = (bf16[3,16,32,384]{3,2,1,0:T(8,128)(2,1)S(1)}, bf16[3,16,32,384]{3,2,1,0:T(8,128)(2,1)}, u32[]{:S(2)}) copy-start(bf16[3,16,32,384]{3,2,1,0:T(8,128)(2,1)} %own_ref.3) | copy-start | bytes 3538948
  1.3 0.7 %copy-start.4 = (s32[3,32,16]{1,2,0:T(8,128)S(1)}, s32[3,32,16]{1,2,0:T(8,128)}, u32[]{:S(2)}) copy-start(s32[3,32,16]{1,2,0:T(8,128)} %param.10) | copy-start | bytes 18436
  4.2 17.1 %collective-permute-start = (bf16[3,8,32,384]{3,2,1,0:T(8,128)(2,1)S(1)}, bf16[3,8,32,384]{3,2,1,0:T(8,128)(2,1)S(1)}, u32[]{:S(2)}, u32[]{:S(2)}) collective-permute-start(bf16[3,8,32,384]{3,2,1,0:T(8,128)(2,1)S(1)} %get-tuple-element.7), channel_id=1, source_target_pairs={{0,1},{1,2},{2,3},{3,4},{4,5},{5,6},{6,7},{7,0},{8,9},{9,10},{10,1... | collective-permute-start | bytes 1769480 | tf_op jit(solution)/shard_map/ppermute | solution.py:202
  4.8 16.5 %collective-permute-start.1 = (bf16[3,8,32,384]{3,2,1,0:T(8,128)(2,1)S(1)}, bf16[3,8,32,384]{3,2,1,0:T(8,128)(2,1)S(1)}, u32[]{:S(2)}, u32[]{:S(2)}) collective-permute-start(bf16[3,8,32,384]{3,2,1,0:T(8,128)(2,1)S(1)} %get-tuple-element.8), channel_id=1, source_target_pairs={{1,0},{2,1},{3,2},{4,3},{5,4},{6,5},{7,6},{0,7},{9,8},{10,9},{11,1... | collective-permute-start | bytes 1769480 | tf_op jit(solution)/shard_map/ppermute | solution.py:203
  10.0 2.8 %copy-start = (bf16[3,32,8,32,128]{4,3,2,1,0:T(8,128)(2,1)S(1)}, bf16[3,32,8,32,128]{4,3,2,1,0:T(8,128)(2,1)}, u32[]{:S(2)}) copy-start(bf16[3,32,8,32,128]{4,3,2,1,0:T(8,128)(2,1)} %weight_ref.1) | copy-start | bytes 18874372
  12.8 1.4 %copy-start.3 = (bf16[200,4096]{1,0:T(8,128)(2,1)S(1)}, bf16[200,4096]{1,0:T(8,128)(2,1)}, u32[]{:S(2)}) copy-start(bf16[200,4096]{1,0:T(8,128)(2,1)} %eof_ref.1) | copy-start | bytes 4915204
  14.3 7.1 %copy-start.2 = (bf16[3,16,32,384]{3,2,1,0:T(8,128)(2,1)S(1)}, bf16[3,16,32,384]{3,2,1,0:T(8,128)(2,1)}, u32[]{:S(2)}) copy-start(bf16[3,16,32,384]{3,2,1,0:T(8,128)(2,1)} %own_ref.3) | copy-start | bytes 3538948

commit v3 on v2

--- a/solution.py
+++ b/solution.py
@@ -26,6 +26,7 @@
     step = pl.program_id(0)
     grids, _, pairs, cells, _ = weight_ref.shape
     modes = eof_ref.shape[0]
+    ways = len(totals) // grids
 
     @pl.when(step == 0)
     def _():
@@ -43,13 +44,16 @@
                 slot = slot_ref[(g * tiles + step * block + t) * pairs + p]
                 where = pl.ds(pl.multiple_of(slot * cells, cells), cells)
                 start = (g * pairs + p) * cells
-                totals[g][where, :modes] += product[start:start + cells]
+                totals[g * ways + p % ways][where, :modes] += product[start:start + cells]
 
     @pl.when(step == pl.num_programs(0) - 1)
     def _():
         height, width = out_ref.shape[1], totals[0].shape[1]
         for g in range(grids):
-            for i, term in enumerate(split_terms(totals[g][:height])):
+            total = totals[g * ways][:height]
+            for way in range(1, ways):
+                total = total + totals[g * ways + way][:height]
+            for i, term in enumerate(split_terms(total)):
                 out_ref[g, :, i * width:(i + 1) * width] = term
 
 
@@ -74,15 +78,18 @@
             lax.fori_loop(0, request_ref.shape[1], place, jnp.int32(0), unroll=True)
 
 
-def project(rel_ref, near_ref, tile_ref, before_ref, own_ref, after_ref, basis_ref, part, source):
+def project(table_ref, before_ref, own_ref, after_ref, basis_ref, part, source):
     grids, _, cells, columns = own_ref.shape
     _, chips, bands, rows, _ = part.shape
-    wanted = rel_ref.shape[0] // grids
+    wanted = basis_ref.shape[1] // cells
+    offset = table_ref.shape[0] - grids * wanted
+    src_tiles = own_ref.shape[1]
     width = basis_ref.shape[2] // 3
     for g in range(grids):
         for j in range(wanted):
-            k = g * wanted + j
-            rel, near, tile = rel_ref[k], near_ref[k], tile_ref[k]
+            code = table_ref[offset + g * wanted + j]
+            rel, index = code // src_tiles, code % src_tiles
+            near, tile = jnp.where(rel == 1, 0, index), jnp.where(rel == 1, index, 0)
             side = jnp.where(rel == 0, before_ref[g, near], after_ref[g, near])
             source[j * cells:(j + 1) * cells] = jnp.where(rel == 1, own_ref[g, tile], side)
         product = lax.dot_general(
@@ -106,7 +113,7 @@
 
 
 def reduce_kernel(
-    rel_ref, near_ref, tile_ref, before_ref, own_ref, after_ref, basis_ref, out_ref,
+    table_ref, before_ref, own_ref, after_ref, basis_ref, out_ref,
     source, part, core_in, plane_sum, plane_in, band_sum, band_in, final, other,
     core_send, core_recv, plane_send, plane_recv, band_send, band_recv, last_send, last_recv,
 ):
@@ -120,9 +127,7 @@
     partners = [mate] + plane + column
     for partner in partners:
         pl.semaphore_signal(barrier, inc=1, device_id=partner, device_id_type=MESH)
-    project(
-        rel_ref, near_ref, tile_ref, before_ref, own_ref, after_ref, basis_ref, part, source
-    )
+    project(table_ref, before_ref, own_ref, after_ref, basis_ref, part, source)
     pl.semaphore_wait(barrier, len(partners))
 
     order = list(range(1, chips)) + [0]
@@ -208,11 +213,10 @@
     earlier = jnp.arange(asked)[None, :] < jnp.arange(asked)[:, None]
     same = (relative[:, :, None] == relative[:, None, :]) & earlier
     rank = jnp.sum(same, axis=2, dtype=jnp.int32)
-    near = jnp.where(relative == 1, 0, rank).reshape(-1)
-    local_tiles = jnp.where(relative == 1, wanted % src_tiles, 0).reshape(-1)
-    relative = relative.reshape(-1)
+    codes = relative * src_tiles + jnp.where(relative == 1, wanted % src_tiles, rank)
     live = jnp.arange(pairs, dtype=jnp.int32) < pair_counts[:, :, None]
     slots = jnp.where(live, pair_slots, asked).reshape(-1)
+    table = jnp.concatenate([slots, codes.reshape(-1)])
 
     halves = 2
     width = halves * LANES
@@ -230,14 +234,14 @@
                 pl.BlockSpec((modes, block * TT), lambda s, _: (0, s)),
             ],
             out_specs=pl.BlockSpec((grids, asked * cells, 3 * width), lambda s, _: (0, 0, 0)),
-            scratch_shapes=[pltpu.VMEM(((asked + 1) * cells, width), jnp.float32)] * grids,
+            scratch_shapes=[pltpu.VMEM(((asked + 1) * cells, width), jnp.float32)] * (2 * grids),
         ),
         compiler_params=pltpu.CompilerParams(vmem_limit_bytes=VMEM_LIMIT),
         cost_estimate=pl.CostEstimate(
             flops=2 * weights.size * modes, bytes_accessed=2 * (weights.size + eofs.size),
             transcendentals=0,
         ),
-    )(slots, weights, eofs)
+    )(table, weights, eofs)
 
     chips = lon_count // 2
     rows = grids * columns // (lat_count * chips)
@@ -246,7 +250,7 @@
     summed = pl.pallas_call(
         reduce_kernel,
         out_shape=jax.ShapeDtypeStruct((rows // 2, modes), jnp.float32),
-        in_specs=[smem, smem, smem, vmem, vmem, vmem, vmem],
+        in_specs=[smem, vmem, vmem, vmem, vmem],
         out_specs=vmem,
         scratch_shapes=[
             pltpu.VMEM((asked * cells, columns), jnp.bfloat16),
@@ -261,7 +265,7 @@
         compiler_params=pltpu.CompilerParams(
             collective_id=0, has_side_effects=True, vmem_limit_bytes=VMEM_LIMIT
         ),
-    )(relative, near, local_tiles, before, fields, after, basis)
+    )(table, before, fields, after, basis)
     return jnp.transpose(summed)
 
 

time: 39.4 us -> 39.4 us (level)
    select_n x2 -> x1, other arithmetic: 1.02 us -> 0.02 us  [shards(): relative = (sector - lon_index + 1 + lon_count) % lon_count]
    dynamic_slice x0 -> x1, other arithmetic: none -> 0.99 us  [shards(): wanted = lax.dynamic_index_in_dim(requests, device, 1, keepdims=False)]
where the time goes in v3:
time: 39.4 us; the launch traced here: 39 us
  Pallas kernels  26.3 us (67%)
  local copies, waits for them, and re-layouts  7.18 us (18%)
  starting transfers between devices  3.48 us (9%)
  other arithmetic  1.99 us (5%)
    pallas_call x1, Pallas kernels, shards(): pl.pallas_call(reduce_kernel, out_shape=jax.ShapeDtypeStruct((rows // 2,...  17.2 us
    pallas_call x1, Pallas kernels, shards(): pl.pallas_call(functools.partial(basis_kernel, block, tiles), out_shape=j...  6.88 us
    unnamed x11, local copies, waits for them, and re-layouts  6.84 us
    ppermute x1, starting transfers between devices, shards(): after = lax.ppermute(downward, 'lon', down)  2.92 us
    pallas_call x1, Pallas kernels, shards(): pl.pallas_call(pack_kernel, out_shape=[packed, packed], in_specs=[smem, v...  2.21 us
    dynamic_slice x1, other arithmetic, shards(): wanted = lax.dynamic_index_in_dim(requests, device, 1, keepdims=False)  0.99 us
  transfers between devices with their start and end apart: 2, of which 0 were waited for; matrix products, arithmetic and copies ran while one was open for 6% of the time, Pallas kernels for 18%

profile of v3, /device:TPU:0, one launch (start us, length us, event | category | flops | bytes accessed | tf_op | source)
XLA Modules:
  0.0 39.0 jit_solution(5243721053739401602)
XLA Ops:
  0.0 0.0 copy-start.1
  0.0 1.3 %copy-done.1 = bf16[3,16,32,384]{3,2,1,0:T(8,128)(2,1)S(1)} copy-done((bf16[3,16,32,384]{3,2,1,0:T(8,128)(2,1)S(1)}, bf16[3,16,32,384]{3,2,1,0:T(8,128)(2,1)}, u32[]{:S(2)}) %copy-start.1) | copy-done | bytes 1179672
  1.3 0.0 copy-start.4
  1.3 0.7 %copy-done.4 = s32[3,32,16]{1,2,0:T(8,128)S(1)} copy-done((s32[3,32,16]{1,2,0:T(8,128)S(1)}, s32[3,32,16]{1,2,0:T(8,128)}, u32[]{:S(2)}) %copy-start.4) | copy-done | bytes 6168
  2.0 2.2 %shard_map.64 = (bf16[3,8,32,384]{3,2,1,0:T(8,128)(2,1)S(1)}, bf16[3,8,32,384]{3,2,1,0:T(8,128)(2,1)S(1)}) custom-call(s32[3,16,32]{2,1,0:T(8,128)S(1)} %bitcast.3, bf16[3,16,32,384]{3,2,1,0:T(8,128)(2,1)S(1)} %copy-done.1), custom_call_target="tpu_custom_call" | custom-call | tf_op jit(solution)/shard_map/pallas_call | solution.py:203
  4.2 0.6 %collective-permute-start = (bf16[3,8,32,384]{3,2,1,0:T(8,128)(2,1)S(1)}, bf16[3,8,32,384]{3,2,1,0:T(8,128)(2,1)S(1)}, u32[]{:S(2)}, u32[]{:S(2)}) collective-permute-start(bf16[3,8,32,384]{3,2,1,0:T(8,128)(2,1)S(1)} %get-tuple-element.7), channel_id=1, source_target_pairs={{0,1},{1,2},{2,3},{3,4},{4,5},{5,6},{6,7},{7,0},{8,9},{9,10},{10,1... | collective-permute-start | bytes 1769480 | tf_op jit(solution)/shard_map/ppermute | solution.py:207
  4.8 2.9 %collective-permute-start.1 = (bf16[3,8,32,384]{3,2,1,0:T(8,128)(2,1)S(1)}, bf16[3,8,32,384]{3,2,1,0:T(8,128)(2,1)S(1)}, u32[]{:S(2)}, u32[]{:S(2)}) collective-permute-start(bf16[3,8,32,384]{3,2,1,0:T(8,128)(2,1)S(1)} %get-tuple-element.8), channel_id=1, source_target_pairs={{1,0},{2,1},{3,2},{4,3},{5,4},{6,5},{7,6},{0,7},{9,8},{10,9},{11,1... | collective-permute-start | bytes 1769480 | tf_op jit(solution)/shard_map/ppermute | solution.py:208
  7.7 1.0 %dynamic-slice_reduce_fusion = (s32[3,16]{1,0:T(4,128)S(1)}, s32[3,16]{1,0:T(4,128)S(1)}) fusion(s32[3,32,16]{1,2,0:T(8,128)} %param.10, s32[]{:T(128)S(6)} %select_n.50, s32[]{:T(128)S(6)} %axis_index.25, s32[]{:T(128)S(6)} %mul.9), kind=kLoop, calls=%fused_computation.16 | loop fusion | flops 1392 | bytes 588 | tf_op jit(solution)/shard_map/jit(dynamic_index_in_dim)/dynamic_slice | solution.py:210
  8.7 0.1 squeeze.6
  8.8 0.2 convert_reduce_fusion
  9.0 0.1 reduce_sum.12
  9.1 0.7 %fusion.7 = s32[3,32,8]{1,2,0:T(8,128)S(1)} fusion(s32[3,32,8]{1,2,0:T(8,128)} %param.8, s32[3,32]{1,0:T(4,128)} %param.9), kind=kLoop, calls=%fused_computation.18 | loop fusion | flops 1536 | bytes 6528 | tf_op jit(solution)/shard_map/jit(_where)/select_n | solution.py:218
  9.8 0.1 copy.8
  9.9 0.1 reshape.61
  10.1 0.0 copy-start
  10.1 2.8 %copy-done = bf16[3,32,8,32,128]{4,3,2,1,0:T(8,128)(2,1)S(1)} copy-done((bf16[3,32,8,32,128]{4,3,2,1,0:T(8,128)(2,1)S(1)}, bf16[3,32,8,32,128]{4,3,2,1,0:T(8,128)(2,1)}, u32[]{:S(2)}) %copy-start) | copy-done | bytes 6291480
  12.9 0.0 copy-start.3
  12.9 1.4 %copy-done.3 = bf16[200,4096]{1,0:T(8,128)(2,1)S(1)} copy-done((bf16[200,4096]{1,0:T(8,128)(2,1)S(1)}, bf16[200,4096]{1,0:T(8,128)(2,1)}, u32[]{:S(2)}) %copy-start.3) | copy-done | bytes 1638424
  14.3 0.0 copy-start.2
  14.3 6.9 %shard_map.65.basis_ref = bf16[3,512,768]{2,1,0:T(8,128)(2,1)S(1)} custom-call(s32[816]{0:T(1024)S(1)} %pad_add_fusion.slot_ref.table_ref, bf16[3,32,8,32,128]{4,3,2,1,0:T(8,128)(2,1)S(1)} %copy-done, bf16[200,4096]{1,0:T(8,128)(2,1)S(1)} %copy-done.3), custom_call_target="tpu_custom_call" | custom-call | flops 1258291200 | bytes 7929856 | tf_op jit(solution)/shard_map/pallas_call | solution.py:226
  21.2 0.0 collective-permute-done.before_ref
  21.2 0.0 collective-permute-done.1.after_ref
  21.2 0.0 copy-done.2
  21.2 17.2 %shard_map.66 = f32[36,200]{1,0:T(8,128)S(1)} custom-call(s32[816]{0:T(1024)S(1)} %pad_add_fusion.slot_ref.table_ref, bf16[3,8,32,384]{3,2,1,0:T(8,128)(2,1)S(1)} %collective-permute-done.before_ref, bf16[3,16,32,384]{3,2,1,0:T(8,128)(2,1)S(1)} %copy-done.2, bf16[3,8,32,384]{3,2,1,0:T(8,128)(2,1)S(1)} %collective-permute-done.1.after_ref, ...), custom_call_target="tpu_custom_call" | custom-call | tf_op jit(solution)/shard_map/pallas_call | solution.py:250
  38.4 0.6 %copy.10 = f32[200,36]{0,1:T(8,128)} copy(f32[200,36]{0,1:T(8,128)S(1)} %bitcast.2) | data formatting | bytes 57600
  (4 shorter events, 0.1 us)
Async XLA Ops:
  0.0 1.3 %copy-start.1 = (bf16[3,16,32,384]{3,2,1,0:T(8,128)(2,1)S(1)}, bf16[3,16,32,384]{3,2,1,0:T(8,128)(2,1)}, u32[]{:S(2)}) copy-start(bf16[3,16,32,384]{3,2,1,0:T(8,128)(2,1)} %own_ref.3) | copy-start | bytes 3538948
  1.3 0.7 %copy-start.4 = (s32[3,32,16]{1,2,0:T(8,128)S(1)}, s32[3,32,16]{1,2,0:T(8,128)}, u32[]{:S(2)}) copy-start(s32[3,32,16]{1,2,0:T(8,128)} %param.10) | copy-start | bytes 18436
  4.2 16.9 %collective-permute-start = (bf16[3,8,32,384]{3,2,1,0:T(8,128)(2,1)S(1)}, bf16[3,8,32,384]{3,2,1,0:T(8,128)(2,1)S(1)}, u32[]{:S(2)}, u32[]{:S(2)}) collective-permute-start(bf16[3,8,32,384]{3,2,1,0:T(8,128)(2,1)S(1)} %get-tuple-element.7), channel_id=1, source_target_pairs={{0,1},{1,2},{2,3},{3,4},{4,5},{5,6},{6,7},{7,0},{8,9},{9,10},{10,1... | collective-permute-start | bytes 1769480 | tf_op jit(solution)/shard_map/ppermute | solution.py:207
  4.8 16.4 %collective-permute-start.1 = (bf16[3,8,32,384]{3,2,1,0:T(8,128)(2,1)S(1)}, bf16[3,8,32,384]{3,2,1,0:T(8,128)(2,1)S(1)}, u32[]{:S(2)}, u32[]{:S(2)}) collective-permute-start(bf16[3,8,32,384]{3,2,1,0:T(8,128)(2,1)S(1)} %get-tuple-element.8), channel_id=1, source_target_pairs={{1,0},{2,1},{3,2},{4,3},{5,4},{6,5},{7,6},{0,7},{9,8},{10,9},{11,1... | collective-permute-start | bytes 1769480 | tf_op jit(solution)/shard_map/ppermute | solution.py:208
  10.1 2.8 %copy-start = (bf16[3,32,8,32,128]{4,3,2,1,0:T(8,128)(2,1)S(1)}, bf16[3,32,8,32,128]{4,3,2,1,0:T(8,128)(2,1)}, u32[]{:S(2)}) copy-start(bf16[3,32,8,32,128]{4,3,2,1,0:T(8,128)(2,1)} %weight_ref.1) | copy-start | bytes 18874372
  12.9 1.4 %copy-start.3 = (bf16[200,4096]{1,0:T(8,128)(2,1)S(1)}, bf16[200,4096]{1,0:T(8,128)(2,1)}, u32[]{:S(2)}) copy-start(bf16[200,4096]{1,0:T(8,128)(2,1)} %eof_ref.1) | copy-start | bytes 4915204
  14.3 6.9 %copy-start.2 = (bf16[3,16,32,384]{3,2,1,0:T(8,128)(2,1)S(1)}, bf16[3,16,32,384]{3,2,1,0:T(8,128)(2,1)}, u32[]{:S(2)}) copy-start(bf16[3,16,32,384]{3,2,1,0:T(8,128)(2,1)} %own_ref.3) | copy-start | bytes 3538948
